TPU v7x, 256 devices: a whole 4x4x8 slice. The times are simulated.
256 devices in a mesh: tile: 64 (over x, z, core), lev: 4 (over y).
Axes of the slice: x: 4, y: 4, z: 8, core: 2. Of those that a mesh axis runs over, the one named last changes fastest.
Arguments:
- mixing: float32 [3, 64, 262144], P(None, 'lev', 'tile'), may hold values from 0.05 to 3
- density: float32 [64, 262144], P('lev', 'tile'), may hold values from 0.4 to 1.2
- routes: int32 [262144, 1], P('tile'), may hold values from 0 to 63; in each aligned block of 4096 rows (0 to 4095, 4096 to 8191, ...) at most 128 rows name the same one
- beam_weight: float32 [64, 168, 64], P('tile'), may hold values from 0.001 to 0.06
- gate_adjoint: float32 [168, 524288], P('lev', 'tile'), may hold values from -6 to 6
Outputs:
- gate_values: float32 [168, 524288], P('lev', 'tile')
- increments: float32 [3, 64, 262144], P(None, 'lev', 'tile')
Inputs may be any that keep to these rules, and one draw needn't show every extreme that they name: `routes`: each column names the site that observes it; the columns of one tile index send at most 128 columns to one site, and exactly 128 to some site.
All inputs are finite; a program needn't handle non-finite values.
Results may differ from a plain program's by a relative error of at most 0.00007.
Values sent between devices are 32-bit elements; how exact they have to be, the bound alone decides.
A program may use at most 64 MiB of HBM per device.

v0:
```python
import jax
import jax.numpy as jnp
from jax import lax
from jax.sharding import PartitionSpec as P

coefficients = (3.63, 0.96, 1.98)
exponents = (1.75, 1.66, 1.75)


def cut_along(value, dim, devices):
    dims = value.shape
    parts = value.reshape(*dims[:dim], devices, dims[dim] // devices, *dims[dim + 1 :])
    return jnp.moveaxis(parts, dim, 0)


def sum_at_owner(value, axis, dim):
    devices = lax.axis_size(axis)
    parts = lax.all_to_all(cut_along(value, dim, devices), axis, 0, 0, tiled=True)
    return jnp.sum(parts, axis=0)


def in_order(parts, dim):
    dims = list(parts.shape[1:])
    dims[dim] *= parts.shape[0]
    return jnp.moveaxis(parts, 0, dim).reshape(dims)


def from_everyone(value, axis):
    devices = lax.axis_size(axis)
    return lax.all_to_all(
        jnp.broadcast_to(value[None], (devices, *value.shape)), axis, 0, 0, tiled=True
    )


def gather_directly(value, axis, dim):
    return in_order(from_everyone(value, axis), dim)


def reflect(mixing, density):
    summed = jnp.zeros(density.shape, jnp.float32)
    slopes = []
    for species in range(3):
        scaled = density * mixing[species]
        powered = coefficients[species] * jnp.exp(exponents[species] * jnp.log(scaled))
        summed = summed + powered
        slopes.append(exponents[species] * powered / mixing[species])
    return (summed, jnp.stack(slopes))


def per_device(mixing, density, routes, beam_weight, gate_adjoint):
    tile_count = lax.axis_size("tile")
    level_count = lax.axis_size("lev")
    level_dev = mixing.shape[1]
    column_dev = mixing.shape[2]
    slot_total = 2 * column_dev
    capacity = slot_total // tile_count
    reflectivity, slopes = reflect(mixing, density)
    target = routes[:, 0]
    onehot = (target[:, None] == jnp.arange(tile_count, dtype=jnp.int32)[None, :]).astype(jnp.int32)
    ranking = jnp.sum((jnp.cumsum(onehot, axis=0) - onehot) * onehot, axis=1)
    position = target * capacity + ranking
    outgoing = jnp.zeros((level_dev, slot_total), jnp.float32).at[:, position].set(reflectivity)
    weights = beam_weight[0]
    level_index = lax.axis_index("lev")
    gate_rows = weights.shape[0] // level_count
    row_weights = lax.dynamic_slice_in_dim(weights, level_index * gate_rows, gate_rows, 0)
    returned = sum_at_owner(
        lax.dot_general(
            row_weights,
            gate_adjoint,
            (((0,), (0,)), ((), ())),
            precision=lax.Precision.HIGHEST,
            preferred_element_type=jnp.float32,
        ),
        "lev",
        0,
    )
    incoming = lax.all_to_all(outgoing, "tile", split_axis=1, concat_axis=1, tiled=True)
    restored = lax.all_to_all(returned, "tile", split_axis=1, concat_axis=1, tiled=True)
    column_levels = gather_directly(incoming, "lev", 0)
    gate_values = jnp.dot(
        row_weights,
        column_levels,
        precision=lax.Precision.HIGHEST,
        preferred_element_type=jnp.float32,
    )
    increments = slopes * restored[:, position][None]
    return (gate_values, increments)


def solution(mesh):
    return jax.shard_map(
        per_device,
        mesh=mesh,
        in_specs=(
            P(None, "lev", "tile"),
            P("lev", "tile"),
            P("tile", None),
            P("tile", None, None),
            P("lev", "tile"),
        ),
        out_specs=(P("lev", "tile"), P(None, "lev", "tile")),
        check_vma=False,
    )
```

profile of v0, /device:TPU:1, one launch (start us, length us, event | category | flops | bytes accessed | tf_op | source)
XLA Modules:
  0.0 159.3 jit_solution(7119846310892743437)
XLA Ops:
  0.6 0.0 copy-start
  0.6 1.0 constant_dynamic-slice_fusion
  1.7 0.4 copy-done
  2.1 3.2 %fusion.2 = f32[4,16,8192]{2,1,0:T(8,128)} fusion(f32[4,16,42]{2,1,0:T(8,128)S(1)} %bitcast.107, f32[42,8192]{1,0:T(8,128)S(1)} %copy-done), kind=kOutput, calls=%fused_computation.4 | convolution fusion | flops 264241152 | bytes 3484160 | tf_op jit(solution)/shard_map/dot_general | solution.py:68
  5.2 5.1 %all-to-all-start.2 = ((f32[4,16,8192]{2,1,0:T(8,128)}), f32[4,16,8192]{2,1,0:T(8,128)}, u32[]{:S(2)}, u32[]{:S(2)}) async-start(f32[4,16,8192]{2,1,0:T(8,128)} %fusion.2), calls=%async_computation.2 | async-start | bytes 4194304 | tf_op jit(solution)/shard_map/all_to_all | solution.py:18
  10.4 1.1 fusion.19
  11.5 1.1 fusion.7
  12.6 32.3 %reduce-window.6 = s32[64,32,128]{2,1,0:T(8,128)S(1)} reduce-window(s32[64,32,128]{2,1,0:T(8,128)} %fusion.7, s32[]{:T(128)} %constant.15.clone.1), window={size=1x1x128 pad=0_0x0_0x127_0}, to_apply=%region_0.0 | reduce-window | flops 33292288 | bytes 2097156 | tf_op jit(solution)/shard_map/reduce-window
  45.0 1.3 slice.25
  46.3 1.7 %copy.30 = s32[64,32,1]{1,0,2:T(8,128)S(1)} copy(s32[64,32,1]{2,1,0:T(8,128)} %slice.25) | data formatting | bytes 16384 | tf_op jit(solution)/shard_map/reshape.1
  47.9 0.2 reduce-window.9
  48.1 2.0 %copy.24 = f32[4096,16]{1,0:T(8,128)} copy(f32[4096,16]{0,1:T(8,128)S(1)} %get-tuple-element.4) | data formatting | bytes 524288 | tf_op jit(solution)/shard_map/add | solution.py:45
  50.1 0.3 broadcast_add_fusion
  50.5 0.9 fusion.6
  51.4 13.1 %scatter_custom_fusion = f32[16,8192]{0,1:T(8,128)} fusion(s32[4096]{0:T(1024)S(1)} %bitcast.113, f32[4096,16]{1,0:T(8,128)} %copy.24, f32[]{:T(128)} %constant.11.clone.1), kind=kCustom, calls=%fused_computation.2 | custom fusion | bytes 524800 | tf_op jit(solution)/shard_map/scatter | solution.py:62
  64.4 3.5 %copy.25 = f32[16,64,128]{2,0,1:T(8,128)} copy(f32[16,64,128]{0,2,1:T(8,128)} %bitcast.103) | data formatting | bytes 1048576 | tf_op jit(solution)/shard_map/all_to_all | solution.py:78
  67.9 0.0 all-to-all-done.2
  68.0 12.4 %all-to-all-start = ((f32[16,64,128]{2,0,1:T(8,128)}), f32[16,64,128]{2,0,1:T(8,128)S(1)}, u32[]{:S(2)}, u32[]{:S(2)}) async-start(f32[16,64,128]{2,0,1:T(8,128)} %copy.25), calls=%async_computation | async-start | bytes 1048576 | tf_op jit(solution)/shard_map/all_to_all | solution.py:78
  80.4 1.8 %reduce_sum.22 = f32[16,8192]{1,0:T(8,128)S(1)} reduce(f32[4,16,8192]{2,1,0:T(8,128)} %all-to-all-done.2, f32[]{:T(128)} %constant.11.clone.1), dimensions={0}, to_apply=%region_4.5 | reduce | flops 393216 | bytes 2621444 | tf_op jit(solution)/shard_map/reduce_sum | solution.py:19
  82.2 0.8 copy_bitcast_fusion.1
  83.0 14.7 %all-to-all-done = f32[16,64,128]{2,0,1:T(8,128)S(1)} async-done(((f32[16,64,128]{2,0,1:T(8,128)}), f32[16,64,128]{2,0,1:T(8,128)S(1)}, u32[]{:S(2)}, u32[]{:S(2)}) %all-to-all-start) | async-done | bytes 524320 | tf_op jit(solution)/shard_map/all_to_all | solution.py:78
  97.7 6.3 %all-to-all-start.3 = ((f32[16,64,128]{2,0,1:T(8,128)}), f32[16,64,128]{2,0,1:T(8,128)S(1)}, u32[]{:S(2)}, u32[]{:S(2)}) async-start(f32[16,64,128]{2,0,1:T(8,128)} %copy_bitcast_fusion.1), calls=%async_computation.3 | async-start | bytes 1048576 | tf_op jit(solution)/shard_map/all_to_all | solution.py:79
  104.0 17.2 %all-to-all-done.3 = f32[16,64,128]{2,0,1:T(8,128)S(1)} async-done(((f32[16,64,128]{2,0,1:T(8,128)}), f32[16,64,128]{2,0,1:T(8,128)S(1)}, u32[]{:S(2)}, u32[]{:S(2)}) %all-to-all-start.3) | async-done | bytes 524320 | tf_op jit(solution)/shard_map/all_to_all | solution.py:79
  121.3 1.5 broadcast_in_dim.8
  122.7 4.6 %all-to-all-start.1 = ((f32[4,16,8192]{2,1,0:T(8,128)}), f32[4,16,8192]{2,1,0:T(8,128)}, u32[]{:S(2)}, u32[]{:S(2)}) async-start(f32[4,16,8192]{2,1,0:T(8,128)} %broadcast_in_dim.8), calls=%async_computation.1 | async-start | bytes 4194304 | tf_op jit(solution)/shard_map/all_to_all | solution.py:30
  127.4 2.6 %copy.28 = f32[16,64,128]{0,2,1:T(8,128)} copy(f32[16,64,128]{2,0,1:T(8,128)S(1)} %all-to-all-done.3) | data formatting | bytes 1048576 | tf_op jit(solution)/shard_map/all_to_all | solution.py:79
  130.0 16.3 %gather_fusion = f32[4096,16]{1,0:T(8,128)} fusion(f32[16,8192]{0,1:T(8,128)} %bitcast.104, s32[4096]{0:T(1024)S(1)} %broadcast_clamp_fusion), kind=kCustom, calls=%fused_computation | custom fusion | bytes 540672 | tf_op jit(solution)/shard_map/gather | solution.py:87
  146.3 2.2 %copy.29 = f32[16,4096]{1,0:T(8,128)S(1)} copy(f32[16,4096]{0,1:T(8,128)} %bitcast.106) | data formatting | bytes 524288 | tf_op jit(solution)/shard_map/gather | solution.py:87
  148.5 5.6 %all-to-all-done.1 = f32[4,16,8192]{2,1,0:T(8,128)} async-done(((f32[4,16,8192]{2,1,0:T(8,128)}), f32[4,16,8192]{2,1,0:T(8,128)}, u32[]{:S(2)}, u32[]{:S(2)}) %all-to-all-start.1) | async-done | bytes 2097184 | tf_op jit(solution)/shard_map/all_to_all | solution.py:30
  154.0 4.3 %fusion.20 = f32[42,8192]{1,0:T(8,128)} fusion(f32[64,8192]{1,0:T(8,128)} %bitcast.13, f32[1,42,64]{1,2,0:T(8,128)S(1)} %constant_dynamic-slice_fusion), kind=kOutput, calls=%fused_computation.37 | convolution fusion | flops 264241152 | bytes 3484160 | tf_op jit(solution)/shard_map/dot_general | solution.py:81
  158.3 0.0 copy-done.2
  158.3 0.9 maximum_multiply_fusion
  (12 shorter events, 0.1 us)
Async XLA Ops:
  0.6 1.4 copy-start
  5.2 5.1 %copy-start.3 = (f32[3,16,4096]{2,1,0:T(8,128)S(1)}, f32[3,16,4096]{2,1,0:T(8,128)}, u32[]{:S(2)}) copy-start(f32[3,16,4096]{2,1,0:T(8,128)} %param.5) | copy-start | bytes 2359300
  5.2 5.1 %copy-start.4 = (f32[16,4096]{1,0:T(8,128)S(1)}, f32[16,4096]{1,0:T(8,128)}, u32[]{:S(2)}) copy-start(f32[16,4096]{1,0:T(8,128)} %param.6) | copy-start | bytes 786436
  5.2 62.7 %all-to-all-start.2 = ((f32[4,16,8192]{2,1,0:T(8,128)}), f32[4,16,8192]{2,1,0:T(8,128)}, u32[]{:S(2)}, u32[]{:S(2)}) async-start(f32[4,16,8192]{2,1,0:T(8,128)} %fusion.2), calls=%async_computation.2 | async-start | bytes 4194304 | tf_op jit(solution)/shard_map/all_to_all | solution.py:18
  10.4 1.2 copy-start.5
  68.0 29.7 %all-to-all-start = ((f32[16,64,128]{2,0,1:T(8,128)}), f32[16,64,128]{2,0,1:T(8,128)S(1)}, u32[]{:S(2)}, u32[]{:S(2)}) async-start(f32[16,64,128]{2,0,1:T(8,128)} %copy.25), calls=%async_computation | async-start | bytes 1048576 | tf_op jit(solution)/shard_map/all_to_all | solution.py:78
  97.7 23.6 %all-to-all-start.3 = ((f32[16,64,128]{2,0,1:T(8,128)}), f32[16,64,128]{2,0,1:T(8,128)S(1)}, u32[]{:S(2)}, u32[]{:S(2)}) async-start(f32[16,64,128]{2,0,1:T(8,128)} %copy_bitcast_fusion.1), calls=%async_computation.3 | async-start | bytes 1048576 | tf_op jit(solution)/shard_map/all_to_all | solution.py:79
  122.7 31.3 %all-to-all-start.1 = ((f32[4,16,8192]{2,1,0:T(8,128)}), f32[4,16,8192]{2,1,0:T(8,128)}, u32[]{:S(2)}, u32[]{:S(2)}) async-start(f32[4,16,8192]{2,1,0:T(8,128)} %broadcast_in_dim.8), calls=%async_computation.1 | async-start | bytes 4194304 | tf_op jit(solution)/shard_map/all_to_all | solution.py:30
  148.5 9.9 %copy-start.1 = (f32[1,16,4096]{2,1,0:T(8,128)S(1)}, f32[1,16,4096]{2,1,0:T(8,128)}, u32[]{:S(2)}) copy-start(f32[1,16,4096]{2,1,0:T(8,128)} %get-tuple-element.3) | copy-start | bytes 786436
  148.5 9.9 %copy-start.2 = (f32[1,16,4096]{2,1,0:T(8,128)S(1)}, f32[1,16,4096]{2,1,0:T(8,128)}, u32[]{:S(2)}) copy-start(f32[1,16,4096]{2,1,0:T(8,128)} %get-tuple-element.5) | copy-start | bytes 786436
where the time goes:
time: 162 us; the launch traced here: 159 us
  local copies, waits for them, and re-layouts  46.4 us (29%)
  other arithmetic  38.7 us (24%)
  waiting for transfers between devices  37.5 us (23%)
  starting transfers between devices  28.5 us (18%)
  matrix products  7.45 us (5%)
    another operation x3, other arithmetic  32.9 us
    gather x2, local copies, waits for them, and re-layouts, per_device(): increments = slopes * restored[:, position][None]  18.5 us
    all_to_all x1, waiting for transfers between devices, per_device(): lax.all_to_all(returned, 'tile', split_axis=1, concat_axis=1, tiled=True)  17.2 us
    all_to_all x1, waiting for transfers between devices, per_device(): lax.all_to_all(outgoing, 'tile', split_axis=1, concat_axis=1, tiled=True)  14.7 us
    scatter x1, local copies, waits for them, and re-layouts, per_device(): jnp.zeros((level_dev, slot_total), jnp.float32).at[:, position]  13.1 us
    all_to_all x1, starting transfers between devices, per_device(): lax.all_to_all(outgoing, 'tile', split_axis=1, concat_axis=1, tiled=True)  12.4 us
    all_to_all x1, starting transfers between devices, per_device(): lax.all_to_all(returned, 'tile', split_axis=1, concat_axis=1, tiled=True)  6.29 us
    all_to_all x1, waiting for transfers between devices, from_everyone(): lax.all_to_all(jnp.broadcast_to(value[None], (devices, *value.shape)), ax...  5.56 us
  transfers between devices with their start and end apart: 4, of which 3 were waited for; matrix products, arithmetic and copies ran while one was open for 51% of the time, Pallas kernels for 0%

commit v1 on v0

v1 whole, which is shorter than its diff:
```python
import jax
import jax.numpy as jnp
from jax import lax
from jax.experimental import pallas as pl
from jax.experimental.pallas import tpu as pltpu
from jax.sharding import PartitionSpec as P

coefficients = (3.63, 0.96, 1.98)
exponents = (1.75, 1.66, 1.75)

MESH = pl.DeviceIdType.MESH
F32 = jnp.float32
BF16 = jnp.bfloat16

NX, NZ, NC = 4, 8, 2
LEVS = 4
TILES = NX * NZ * NC
PAIRS = NX * NZ
CHUNKS = 4
PC = PAIRS // CHUNKS
HALF = PC // 2
COLS = 4096
LD = 16
LEV = 64
CAP = 128
GR = 42


def split2(value):
    hi = value.astype(BF16)
    lo = (value - hi.astype(F32)).astype(BF16)
    return hi, lo


def dot(a, b, dims=((1,), (0,))):
    return lax.dot_general(a, b, (dims, ((), ())), preferred_element_type=F32)


def shift_of(kp):
    dzi = kp // NX
    dx = kp % NX
    dz = ((dzi + 1) // 2) * (2 * (dzi % 2) - 1)
    return dx, dz


def kernel(
    mixing_hbm, density_hbm, routes_hbm, weight_hbm, adjoint_hbm,
    gate_hbm, incr_hbm,
    mixing, density, target, weight, adjoint, gate, incr,
    slopes, parts, onehot, prefix, ranks1h, lhs, out_blocks,
    partial, rs1, rs2, final, back, cols, restored,
    in_sem, out_sem, a2a_send, a2a_recv, bk_send, bk_recv,
    rs1_send, rs1_recv, rs2_send, rs2_recv, ag1_send, ag1_recv, ag2_send, ag2_recv,
):
    tile = lax.axis_index("tile")
    lev = lax.axis_index("lev")
    core = tile % NC
    zz = (tile // NC) % NZ
    xx = tile // (NC * NZ)
    right = (lev + 1) % LEVS
    left = (lev + 3) % LEVS
    across = (lev + 2) % LEVS

    def pair_plus(kp):
        dx, dz = shift_of(kp)
        return ((xx + dx) % NX) * NZ + (zz + dz + NZ) % NZ

    def pair_minus(kp):
        dx, dz = shift_of(kp)
        return ((xx - dx + NX) % NX) * NZ + (zz - dz + NZ) % NZ

    loads = [
        pltpu.make_async_copy(weight_hbm.at[0], weight, in_sem.at[0]),
        pltpu.make_async_copy(adjoint_hbm, adjoint, in_sem.at[1]),
        pltpu.make_async_copy(routes_hbm, target, in_sem.at[2]),
        pltpu.make_async_copy(density_hbm, density, in_sem.at[3]),
        pltpu.make_async_copy(mixing_hbm, mixing, in_sem.at[4]),
    ]
    for load in loads:
        load.start()

    barrier = pltpu.get_barrier_semaphore()

    @pl.loop(1, TILES)
    def _(k):
        pl.semaphore_signal(
            barrier, inc=1, device_id={"tile": (tile + k) % TILES}, device_id_type=MESH
        )

    for peer in (left, right):
        pl.semaphore_signal(barrier, inc=1, device_id={"lev": peer}, device_id_type=MESH)

    loads[0].wait()
    rows = jnp.zeros((GR, LEV), F32)
    for k in range(LEVS):
        rows = jnp.where(lev == k, weight[GR * k : GR * (k + 1), :], rows)
    rows_hi, rows_lo = split2(rows)
    loads[1].wait()

    @pl.loop(0, PAIRS)
    def _(kp):
        at = pl.multiple_of(pair_plus(kp) * 2 * CAP, 2 * CAP)
        g_hi, g_lo = split2(adjoint[:, pl.ds(at, 2 * CAP)])
        tn = ((0,), (0,))
        part = dot(rows_hi, g_hi, tn) + dot(rows_hi, g_lo, tn) + dot(rows_lo, g_hi, tn)
        for k in range(LEVS):
            for c in range(NC):
                partial[k, kp * NC + c] = part[LD * k : LD * (k + 1), CAP * c : CAP * (c + 1)]

    pl.semaphore_wait(barrier, TILES - 1 + 2)

    def lev_copy(src, dst, send, recv, peer):
        return pltpu.make_async_remote_copy(
            src_ref=src, dst_ref=dst, send_sem=send, recv_sem=recv,
            device_id={"lev": peer}, device_id_type=MESH,
        )

    def rs1_copy(c, way):
        at = c * PC + way * HALF
        return lev_copy(
            partial.at[across, pl.ds(at * NC, HALF * NC)], rs1.at[way, c],
            rs1_send.at[way, c], rs1_recv.at[way, c], (right, left)[way],
        )

    def rs2_copy(c, way):
        peer = (right, left)[way]
        return lev_copy(
            partial.at[peer, pl.ds(c * PC * NC, PC * NC)], rs2.at[way, c],
            rs2_send.at[way, c], rs2_recv.at[way, c], peer,
        )

    def ag1_copy(c, way):
        here = cols.at[lev, pl.ds(c * PC * NC, PC * NC)]
        return lev_copy(
            here, here, ag1_send.at[way, c], ag1_recv.at[way, c], (right, left)[way]
        )

    def ag2_copy(c, way):
        here = cols.at[(left, right)[way], pl.ds((c * PC + way * HALF) * NC, HALF * NC)]
        return lev_copy(
            here, here, ag2_send.at[way, c], ag2_recv.at[way, c], (right, left)[way]
        )

    def rs_first(c):
        for way in range(2):
            rs1_copy(c, way).start()

    def rs_second(c):
        for way in range(2):
            rs1_copy(c, way).wait_recv()
            peer = (right, left)[way]
            at = pl.ds((c * PC + way * HALF) * NC, HALF * NC)
            partial[peer, at] = partial[peer, at] + rs1[way, c]
        for way in range(2):
            rs2_copy(c, way).start()

    def back_copy(kp, c, cs):
        return pltpu.make_async_remote_copy(
            src_ref=final.at[kp * NC + cs], dst_ref=back.at[kp * NC + core],
            send_sem=bk_send, recv_sem=bk_recv.at[c],
            device_id={"tile": pair_plus(kp) * NC + cs}, device_id_type=MESH,
        )

    def out_copy(kp, c, cd):
        return pltpu.make_async_remote_copy(
            src_ref=out_blocks.at[kp * NC + cd], dst_ref=cols.at[lev, kp * NC + core],
            send_sem=a2a_send, recv_sem=a2a_recv.at[c],
            device_id={"tile": pair_minus(kp) * NC + cd}, device_id_type=MESH,
        )

    def exchange(copy_of, c):
        if c == 0:
            copy_of(0, 0, 1 - core).start()

        @pl.loop(c * PC + (1 if c == 0 else 0), (c + 1) * PC)
        def _(kp):
            for other in range(NC):
                copy_of(kp, c, other).start()

    def blocks(buf, count, send, recv):
        some = buf.at[pl.ds(0, count)]
        return pltpu.make_async_remote_copy(
            src_ref=some, dst_ref=some, send_sem=send, recv_sem=recv,
            device_id={"lev": right}, device_id_type=MESH,
        )

    def in_chunk(c):
        return PC * NC - (1 if c == 0 else 0)

    def rs_final(c):
        for way in range(2):
            rs2_copy(c, way).wait_recv()
        at = pl.ds(c * PC * NC, PC * NC)
        final[at] = partial[lev, at] + rs2[0, c] + rs2[1, c]

    for c in range(CHUNKS):
        rs_first(c)

    loads[2].wait()
    for j in range(COLS // CAP):
        names = lax.broadcasted_iota(jnp.int32, (TILES, CAP), 0)
        onehot[TILES * j : TILES * (j + 1), :] = jnp.where(
            target[:, CAP * j : CAP * (j + 1)] == names, 1.0, 0.0
        ).astype(BF16)
    upto = jnp.where(
        lax.broadcasted_iota(jnp.int32, (CAP, 2 * CAP), 0)
        < lax.broadcasted_iota(jnp.int32, (CAP, 2 * CAP), 1),
        1.0, 0.0,
    ).astype(BF16)
    prefix[...] = dot(onehot[...], upto)
    carry = jnp.zeros((TILES, CAP), F32)
    slot = lax.broadcasted_iota(jnp.int32, (CAP, CAP), 0).astype(F32)
    for j in range(COLS // CAP):
        at = slice(TILES * j, TILES * (j + 1))
        mine = onehot[at, :].astype(F32) * (prefix[at, :CAP] + carry)
        rank = jnp.sum(mine, axis=0, keepdims=True)
        ranks1h[:, CAP * j : CAP * (j + 1)] = jnp.where(rank == slot, 1.0, 0.0).astype(BF16)
        carry = carry + prefix[at, CAP:]

    rs_second(0)

    loads[3].wait()
    loads[4].wait()
    wide = 512

    @pl.loop(0, COLS // wide)
    def _(j):
        at = pl.ds(pl.multiple_of(j * wide, wide), wide)
        dens = density[:, at]
        summed = jnp.zeros((LD, wide), F32)
        for species in range(3):
            mix = mixing[species, :, at]
            powered = coefficients[species] * jnp.exp(exponents[species] * jnp.log(dens * mix))
            summed = summed + powered
            slopes[species, :, at] = exponents[species] * powered / mix
        hi, lo = split2(summed)
        parts[0, :, at] = hi
        parts[1, :, at] = lo

    rs_second(1)

    def scatter(c):
        @pl.loop(0, PC)
        def _(i):
            pair = pair_minus(c * PC + i)
            for cd in range(NC):
                named = jnp.broadcast_to(target[...], (LD, COLS)) == pair * NC + cd
                mask = jnp.where(named, 1.0, 0.0).astype(BF16)
                at = pl.ds(pl.multiple_of((i * NC + cd) * LD, LD), LD)
                lhs[at, :COLS] = mask * parts[0]
                lhs[at, COLS:] = mask * parts[1]

        nt = ((1,), (1,))
        placed = dot(lhs[:, :COLS], ranks1h[...], nt) + dot(lhs[:, COLS:], ranks1h[...], nt)
        for i in range(PC):
            for cd in range(NC):
                at = (i * NC + cd) * LD
                out_blocks[(c * PC + i) * NC + cd] = placed[at : at + LD]
        if c == 0:
            cols[lev, core] = out_blocks[core]

    for c in range(CHUNKS):
        scatter(c)
        exchange(out_copy, c)
        if c < 2:
            rs_second(c + 2)
        else:
            rs_final(c - 2)
    exchange(back_copy, 0)
    exchange(back_copy, 1)

    def ag_first(c):
        blocks(out_blocks, in_chunk(c), a2a_send, a2a_recv.at[c]).wait_recv()
        for way in range(2):
            ag1_copy(c, way).start()

    def ag_second(c):
        for way in range(2):
            ag1_copy(c, way).wait_recv()
        for way in range(2):
            ag2_copy(c, way).start()

    def gates(c):
        for way in range(2):
            ag2_copy(c, way).wait_recv()

        @pl.loop(c * PC, (c + 1) * PC)
        def _(kp):
            both = [cols[:, kp * NC + cs].reshape(LEV, CAP) for cs in range(NC)]
            x_hi, x_lo = split2(jnp.concatenate(both, axis=1))
            at = pl.multiple_of(pair_plus(kp) * 2 * CAP, 2 * CAP)
            gate[:, pl.ds(at, 2 * CAP)] = (
                dot(rows_hi, x_hi) + dot(rows_hi, x_lo) + dot(rows_lo, x_hi)
            )

    def gather(c):
        blocks(final, in_chunk(c), bk_send, bk_recv.at[c]).wait_recv()
        if c == 0:
            back[core] = final[core]
        span = PC * NC * LD
        b_hi, b_lo = split2(back[c * PC * NC : (c + 1) * PC * NC].reshape(span, CAP))
        lhs[:, :CAP] = b_hi
        lhs[:, CAP : 2 * CAP] = b_lo

        @pl.loop(0, COLS // wide)
        def _(j):
            at = pl.ds(pl.multiple_of(j * wide, wide), wide)
            pick = ranks1h[:, at]
            spread = dot(lhs[:, : 2 * CAP], jnp.concatenate([pick, pick], axis=0))
            names = jnp.broadcast_to(target[:, at], (LD, wide))
            if c == 0:
                total = jnp.zeros((LD, wide), F32)
            else:
                total = restored[:, at]
            for i in range(PC):
                pair = pair_minus(c * PC + i)
                for cd in range(NC):
                    mine = spread[(i * NC + cd) * LD : (i * NC + cd + 1) * LD]
                    total = total + jnp.where(names == pair * NC + cd, mine, 0.0)
            if c < CHUNKS - 1:
                restored[:, at] = total
            else:
                for species in range(3):
                    incr[species, :, at] = slopes[species, :, at] * total

    ag_first(0)
    rs_final(2)
    exchange(back_copy, 2)
    ag_first(1)
    ag_second(0)
    rs_final(3)
    exchange(back_copy, 3)
    ag_first(2)
    ag_second(1)
    gates(0)
    gather(0)
    ag_first(3)
    ag_second(2)
    gates(1)
    gather(1)
    ag_second(3)
    gates(2)
    gather(2)
    gather(3)
    inc_out = pltpu.make_async_copy(incr, incr_hbm, out_sem.at[0])
    inc_out.start()
    gates(3)
    gate_out = pltpu.make_async_copy(gate, gate_hbm, out_sem.at[1])
    gate_out.start()

    for c in range(CHUNKS):
        for way in range(2):
            for copy in (rs1_copy, rs2_copy, ag1_copy, ag2_copy):
                copy(c, way).wait_send()
    blocks(out_blocks, TILES - 1, a2a_send, a2a_recv.at[0]).wait_send()
    blocks(final, TILES - 1, bk_send, bk_recv.at[0]).wait_send()
    inc_out.wait()
    gate_out.wait()


def per_device(mixing, density, routes, beam_weight, gate_adjoint):
    dma = pltpu.SemaphoreType.DMA
    block = (LD, CAP)
    per_way = (2, CHUNKS)
    return pl.pallas_call(
        kernel,
        out_shape=(
            jax.ShapeDtypeStruct((GR, TILES * CAP), F32),
            jax.ShapeDtypeStruct((3, LD, COLS), F32),
        ),
        in_specs=[pl.BlockSpec(memory_space=pl.ANY)] * 5,
        out_specs=[pl.BlockSpec(memory_space=pl.ANY)] * 2,
        scratch_shapes=[
            pltpu.VMEM((3, LD, COLS), F32),
            pltpu.VMEM((LD, COLS), F32),
            pltpu.VMEM((1, COLS), jnp.int32),
            pltpu.VMEM((GR * LEVS, LEV), F32),
            pltpu.VMEM((GR, TILES * CAP), F32),
            pltpu.VMEM((GR, TILES * CAP), F32),
            pltpu.VMEM((3, LD, COLS), F32),
            pltpu.VMEM((3, LD, COLS), F32),
            pltpu.VMEM((2, LD, COLS), BF16),
            pltpu.VMEM((TILES * COLS // CAP, CAP), BF16),
            pltpu.VMEM((TILES * COLS // CAP, 2 * CAP), F32),
            pltpu.VMEM((CAP, COLS), BF16),
            pltpu.VMEM((PC * NC * LD, 2 * COLS), BF16),
            pltpu.VMEM((TILES, *block), F32),
            pltpu.VMEM((LEVS, TILES, *block), F32),
            pltpu.VMEM((2, CHUNKS, HALF * NC, *block), F32),
            pltpu.VMEM((2, CHUNKS, PC * NC, *block), F32),
            pltpu.VMEM((TILES, *block), F32),
            pltpu.VMEM((TILES, *block), F32),
            pltpu.VMEM((LEVS, TILES, *block), F32),
            pltpu.VMEM((LD, COLS), F32),
            dma((5,)), dma((2,)), dma, dma((CHUNKS,)), dma, dma((CHUNKS,)),
            dma(per_way), dma(per_way), dma(per_way), dma(per_way),
            dma(per_way), dma(per_way), dma(per_way), dma(per_way),
        ],
        compiler_params=pltpu.CompilerParams(
            collective_id=0, has_side_effects=True, vmem_limit_bytes=48 * 1024 * 1024
        ),
    )(mixing, density, routes.reshape(1, COLS), beam_weight, gate_adjoint)


def solution(mesh):
    return jax.shard_map(
        per_device,
        mesh=mesh,
        in_specs=(
            P(None, "lev", "tile"),
            P("lev", "tile"),
            P("tile", None),
            P("tile", None, None),
            P("lev", "tile"),
        ),
        out_specs=(P("lev", "tile"), P(None, "lev", "tile")),
        check_vma=False,
    )
```

time: 162 us -> 68.9 us (0.43); the launches traced: 159 us -> 68.6 us
  Pallas kernels: 0 us -> 60.8 us
  local copies, waits for them, and re-layouts: 46.4 us -> 7.16 us
  other arithmetic: 38.7 us -> 0 us
  waiting for transfers between devices: 37.5 us -> 0 us
  starting transfers between devices: 28.5 us -> 0 us
  matrix products: 7.45 us -> 0 us
    pallas_call x0 -> x1, Pallas kernels: none -> 60.8 us  [per_device(): pl.pallas_call(kernel, out_shape=(jax.ShapeDtypeStruct((GR, TILES * CAP),...]
    all_to_all x4 -> x0, waiting for transfers between devices: 37.5 us -> none  [the longest x1 17.2 us: per_device(): lax.all_to_all(returned, 'tile', split_axis=1, concat_axis=1, tiled=True)]
    another operation x4 -> x0, other arithmetic: 34 us -> none
    all_to_all x4 -> x0, starting transfers between devices: 28.5 us -> none  [the longest x1 12.4 us: per_device(): lax.all_to_all(outgoing, 'tile', split_axis=1, concat_axis=1, tiled=True)]
    gather x2 -> x0, local copies, waits for them, and re-layouts: 18.5 us -> none  [per_device(): increments = slopes * restored[:, position][None]]
    scatter x1 -> x0, local copies, waits for them, and re-layouts: 13.1 us -> none  [per_device(): jnp.zeros((level_dev, slot_total), jnp.float32).at[:, position]]
    dot_general x2 -> x0, matrix products: 7.45 us -> none  [the longest x1 4.28 us: per_device(): jnp.dot(row_weights, column_levels, precision=lax.Precision.HIGHEST, pref...]
    all_to_all x3 -> x0, local copies, waits for them, and re-layouts: 6.94 us -> none  [the longest x1 3.5 us: per_device(): lax.all_to_all(outgoing, 'tile', split_axis=1, concat_axis=1, tiled=True)]
  transfers between devices with their start and end apart: 4 -> 0, of which waited for: 3 -> 0; matrix products, arithmetic and copies ran while one was open for 51% -> 0% of each run, Pallas kernels for 0% -> 0%
where the time goes in v1:
time: 68.9 us; the launch traced here: 68.6 us
  Pallas kernels  60.8 us (88%)
  local copies, waits for them, and re-layouts  7.16 us (10%)
    pallas_call x1, Pallas kernels, per_device(): pl.pallas_call(kernel, out_shape=(jax.ShapeDtypeStruct((GR, TILES * CAP),...  60.8 us
    unnamed x11, local copies, waits for them, and re-layouts  7.16 us

profile of v1, /device:TPU:1, one launch (start us, length us, event | category | flops | bytes accessed | tf_op | source)
XLA Modules:
  0.0 68.6 jit_solution(11253936476570873570)
XLA Ops:
  0.6 0.9 %copy.7.weight_hbm = f32[1,168,64]{2,1,0:T(8,128)S(1)} copy(f32[1,168,64]{1,2,0:T(8,128)} %param.8) | data formatting | bytes 86016 | tf_op args[3]
  1.6 0.0 copy-start
  1.6 1.4 %copy-done = f32[42,8192]{1,0:T(8,128)S(1)} copy-done((f32[42,8192]{1,0:T(8,128)S(1)}, f32[42,8192]{1,0:T(8,128)}, u32[]{:S(2)}) %copy-start) | copy-done | bytes 1376280
  3.0 0.0 copy-start.1
  3.0 1.1 %copy-done.1 = f32[3,16,4096]{2,1,0:T(8,128)S(1)} copy-done((f32[3,16,4096]{2,1,0:T(8,128)S(1)}, f32[3,16,4096]{2,1,0:T(8,128)}, u32[]{:S(2)}) %copy-start.1) | copy-done | bytes 786456
  4.1 0.0 copy-start.2
  4.1 0.9 %copy-done.2 = f32[16,4096]{1,0:T(8,128)S(1)} copy-done((f32[16,4096]{1,0:T(8,128)S(1)}, f32[16,4096]{1,0:T(8,128)}, u32[]{:S(2)}) %copy-start.2) | copy-done | bytes 262168
  5.1 0.0 copy-start.3
  5.1 0.7 %copy-done.3 = s32[4096,1]{0,1:T(1,128)S(1)} copy-done((s32[4096,1]{0,1:T(1,128)S(1)}, s32[4096,1]{0,1:T(1,128)}, u32[]{:S(2)}) %copy-start.3) | copy-done | bytes 16408
  5.8 60.8 %shard_map.68 = (f32[42,8192]{1,0:T(8,128)S(1)}, f32[3,16,4096]{2,1,0:T(8,128)S(1)}) custom-call(f32[3,16,4096]{2,1,0:T(8,128)S(1)} %copy-done.1, f32[16,4096]{1,0:T(8,128)S(1)} %copy-done.2, s32[1,4096]{1,0:T(1,128)S(1)} %bitcast.1, f32[1,168,64]{2,1,0:T(8,128)S(1)} %copy.7.weight_hbm, f32[42,8192]{1,0:T(8,128)S(1)} %copy-done), custom_call_target="tpu_custom_call" | custom-call | tf_op jit(solution)/shard_map/pallas_call | solution.py:365
  66.6 1.1 %copy.10 = f32[42,8192]{1,0:T(8,128)} copy(f32[42,8192]{1,0:T(8,128)S(1)} %get-tuple-element.4) | data formatting | bytes 2752512
  67.7 0.9 %copy.11 = f32[3,16,4096]{2,1,0:T(8,128)} copy(f32[3,16,4096]{2,1,0:T(8,128)S(1)} %get-tuple-element.5) | data formatting | bytes 1572864
Async XLA Ops:
  1.6 1.4 %copy-start = (f32[42,8192]{1,0:T(8,128)S(1)}, f32[42,8192]{1,0:T(8,128)}, u32[]{:S(2)}) copy-start(f32[42,8192]{1,0:T(8,128)} %adjoint_hbm.1) | copy-start | bytes 4128772
  3.0 1.1 %copy-start.1 = (f32[3,16,4096]{2,1,0:T(8,128)S(1)}, f32[3,16,4096]{2,1,0:T(8,128)}, u32[]{:S(2)}) copy-start(f32[3,16,4096]{2,1,0:T(8,128)} %mixing_hbm.1) | copy-start | bytes 2359300
  4.1 0.9 %copy-start.2 = (f32[16,4096]{1,0:T(8,128)S(1)}, f32[16,4096]{1,0:T(8,128)}, u32[]{:S(2)}) copy-start(f32[16,4096]{1,0:T(8,128)} %density_hbm.1) | copy-start | bytes 786436
  5.1 0.7 %copy-start.3 = (s32[4096,1]{0,1:T(1,128)S(1)}, s32[4096,1]{0,1:T(1,128)}, u32[]{:S(2)}) copy-start(s32[4096,1]{0,1:T(1,128)} %param.7) | copy-start | bytes 49156

commit v2 on v1

--- a/solution.py
+++ b/solution.py
@@ -45,11 +45,11 @@
 
 def kernel(
     mixing_hbm, density_hbm, routes_hbm, weight_hbm, adjoint_hbm,
-    gate_hbm, incr_hbm,
-    mixing, density, target, weight, adjoint, gate, incr,
+    gate, incr,
+    mixing, density, target, weight, adjoint, pair_of,
     slopes, parts, onehot, prefix, ranks1h, lhs, out_blocks,
-    partial, rs1, rs2, final, back, cols, restored,
-    in_sem, out_sem, a2a_send, a2a_recv, bk_send, bk_recv,
+    partial, rs1, rs2, final, back, cols, restored, got,
+    in_sem, a2a_send, a2a_recv, bk_send, bk_recv,
     rs1_send, rs1_recv, rs2_send, rs2_recv, ag1_send, ag1_recv, ag2_send, ag2_recv,
 ):
     tile = lax.axis_index("tile")
@@ -91,18 +91,19 @@
         pl.semaphore_signal(barrier, inc=1, device_id={"lev": peer}, device_id_type=MESH)
 
     loads[0].wait()
-    rows = jnp.zeros((GR, LEV), F32)
-    for k in range(LEVS):
-        rows = jnp.where(lev == k, weight[GR * k : GR * (k + 1), :], rows)
-    rows_hi, rows_lo = split2(rows)
+    mine = weight[:, :GR]
+    for k in range(1, LEVS):
+        mine = jnp.where(lev == k, weight[:, GR * k : GR * (k + 1)], mine)
+    mine_hi, mine_lo = split2(mine)
+    rows_hi, rows_lo = split2(mine.T)
+    rows3 = jnp.concatenate([rows_hi, rows_hi, rows_lo], axis=1)
     loads[1].wait()
 
-    @pl.loop(0, PAIRS)
+    @pl.loop(0, PAIRS, unroll=4)
     def _(kp):
         at = pl.multiple_of(pair_plus(kp) * 2 * CAP, 2 * CAP)
         g_hi, g_lo = split2(adjoint[:, pl.ds(at, 2 * CAP)])
-        tn = ((0,), (0,))
-        part = dot(rows_hi, g_hi, tn) + dot(rows_hi, g_lo, tn) + dot(rows_lo, g_hi, tn)
+        part = dot(mine_hi, g_hi) + dot(mine_hi, g_lo) + dot(mine_lo, g_hi)
         for k in range(LEVS):
             for c in range(NC):
                 partial[k, kp * NC + c] = part[LD * k : LD * (k + 1), CAP * c : CAP * (c + 1)]
@@ -209,13 +210,16 @@
     ).astype(BF16)
     prefix[...] = dot(onehot[...], upto)
     carry = jnp.zeros((TILES, CAP), F32)
-    slot = lax.broadcasted_iota(jnp.int32, (CAP, CAP), 0).astype(F32)
+    slot = lax.broadcasted_iota(jnp.int32, (NC * CAP, CAP), 0).astype(F32)
     for j in range(COLS // CAP):
         at = slice(TILES * j, TILES * (j + 1))
-        mine = onehot[at, :].astype(F32) * (prefix[at, :CAP] + carry)
-        rank = jnp.sum(mine, axis=0, keepdims=True)
+        before = onehot[at, :].astype(F32) * (prefix[at, :CAP] + carry)
+        odd = (target[:, CAP * j : CAP * (j + 1)] % NC).astype(F32)
+        rank = jnp.sum(before, axis=0, keepdims=True) + CAP * odd
         ranks1h[:, CAP * j : CAP * (j + 1)] = jnp.where(rank == slot, 1.0, 0.0).astype(BF16)
         carry = carry + prefix[at, CAP:]
+
+    pair_of[...] = jnp.broadcast_to((target[...] // NC).astype(F32), (LD, COLS)).astype(BF16)
 
     rs_second(0)
 
@@ -223,7 +227,7 @@
     loads[4].wait()
     wide = 512
 
-    @pl.loop(0, COLS // wide)
+    @pl.loop(0, COLS // wide, unroll=2)
     def _(j):
         at = pl.ds(pl.multiple_of(j * wide, wide), wide)
         dens = density[:, at]
@@ -240,22 +244,21 @@
     rs_second(1)
 
     def scatter(c):
-        @pl.loop(0, PC)
-        def _(i):
+        zero = jnp.zeros((), BF16)
+        for i in range(PC):
             pair = pair_minus(c * PC + i)
-            for cd in range(NC):
-                named = jnp.broadcast_to(target[...], (LD, COLS)) == pair * NC + cd
-                mask = jnp.where(named, 1.0, 0.0).astype(BF16)
-                at = pl.ds(pl.multiple_of((i * NC + cd) * LD, LD), LD)
-                lhs[at, :COLS] = mask * parts[0]
-                lhs[at, COLS:] = mask * parts[1]
-
-        nt = ((1,), (1,))
-        placed = dot(lhs[:, :COLS], ranks1h[...], nt) + dot(lhs[:, COLS:], ranks1h[...], nt)
+            named = pair_of[...] == pair.astype(F32).astype(BF16)
+            for p in range(2):
+                at = (p * PC + i) * LD
+                lhs[at : at + LD, :] = jnp.where(named, parts[p], zero)
+
+        both = dot(lhs[...], ranks1h[...], ((1,), (1,)))
+        placed = both[: PC * LD] + both[PC * LD :]
         for i in range(PC):
             for cd in range(NC):
-                at = (i * NC + cd) * LD
-                out_blocks[(c * PC + i) * NC + cd] = placed[at : at + LD]
+                out_blocks[(c * PC + i) * NC + cd] = placed[
+                    i * LD : (i + 1) * LD, cd * CAP : (cd + 1) * CAP
+                ]
         if c == 0:
             cols[lev, core] = out_blocks[core]
 
@@ -284,39 +287,39 @@
         for way in range(2):
             ag2_copy(c, way).wait_recv()
 
-        @pl.loop(c * PC, (c + 1) * PC)
+        @pl.loop(c * PC, (c + 1) * PC, unroll=4)
         def _(kp):
             both = [cols[:, kp * NC + cs].reshape(LEV, CAP) for cs in range(NC)]
             x_hi, x_lo = split2(jnp.concatenate(both, axis=1))
             at = pl.multiple_of(pair_plus(kp) * 2 * CAP, 2 * CAP)
-            gate[:, pl.ds(at, 2 * CAP)] = (
-                dot(rows_hi, x_hi) + dot(rows_hi, x_lo) + dot(rows_lo, x_hi)
+            gate[:, pl.ds(at, 2 * CAP)] = dot(
+                rows3, jnp.concatenate([x_hi, x_lo, x_hi], axis=0)
             )
 
     def gather(c):
         blocks(final, in_chunk(c), bk_send, bk_recv.at[c]).wait_recv()
         if c == 0:
             back[core] = final[core]
-        span = PC * NC * LD
-        b_hi, b_lo = split2(back[c * PC * NC : (c + 1) * PC * NC].reshape(span, CAP))
-        lhs[:, :CAP] = b_hi
-        lhs[:, CAP : 2 * CAP] = b_lo
+        span = PC * LD
+        for i in range(PC):
+            two = [back[(c * PC + i) * NC + cd] for cd in range(NC)]
+            b_hi, b_lo = split2(jnp.concatenate(two, axis=1))
+            got[i * LD : (i + 1) * LD, :] = b_hi
+            got[span + i * LD : span + (i + 1) * LD, :] = b_lo
 
         @pl.loop(0, COLS // wide)
         def _(j):
             at = pl.ds(pl.multiple_of(j * wide, wide), wide)
-            pick = ranks1h[:, at]
-            spread = dot(lhs[:, : 2 * CAP], jnp.concatenate([pick, pick], axis=0))
-            names = jnp.broadcast_to(target[:, at], (LD, wide))
+            twice = dot(got[...], ranks1h[:, at])
+            spread = twice[:span] + twice[span:]
+            names = jnp.broadcast_to(target[:, at] // NC, (LD, wide))
             if c == 0:
                 total = jnp.zeros((LD, wide), F32)
             else:
                 total = restored[:, at]
             for i in range(PC):
-                pair = pair_minus(c * PC + i)
-                for cd in range(NC):
-                    mine = spread[(i * NC + cd) * LD : (i * NC + cd + 1) * LD]
-                    total = total + jnp.where(names == pair * NC + cd, mine, 0.0)
+                mine = spread[i * LD : (i + 1) * LD]
+                total = jnp.where(names == pair_minus(c * PC + i), mine, total)
             if c < CHUNKS - 1:
                 restored[:, at] = total
             else:
@@ -342,11 +345,7 @@
     gates(2)
     gather(2)
     gather(3)
-    inc_out = pltpu.make_async_copy(incr, incr_hbm, out_sem.at[0])
-    inc_out.start()
     gates(3)
-    gate_out = pltpu.make_async_copy(gate, gate_hbm, out_sem.at[1])
-    gate_out.start()
 
     for c in range(CHUNKS):
         for way in range(2):
@@ -354,36 +353,46 @@
                 copy(c, way).wait_send()
     blocks(out_blocks, TILES - 1, a2a_send, a2a_recv.at[0]).wait_send()
     blocks(final, TILES - 1, bk_send, bk_recv.at[0]).wait_send()
-    inc_out.wait()
-    gate_out.wait()
+
+
+def store(gate, incr, gate_hbm, incr_hbm, sem):
+    copies = [
+        pltpu.make_async_copy(gate, gate_hbm, sem.at[0]),
+        pltpu.make_async_copy(incr, incr_hbm, sem.at[1]),
+    ]
+    for copy in copies:
+        copy.start()
+    for copy in copies:
+        copy.wait()
 
 
 def per_device(mixing, density, routes, beam_weight, gate_adjoint):
     dma = pltpu.SemaphoreType.DMA
     block = (LD, CAP)
     per_way = (2, CHUNKS)
-    return pl.pallas_call(
+    gate_shape, incr_shape = (GR, TILES * CAP), (3, LD, COLS)
+    operands = (
+        mixing, density, routes.reshape(1, COLS),
+        jnp.swapaxes(beam_weight, 1, 2), gate_adjoint,
+    )
+    gate, incr = pl.pallas_call(
         kernel,
-        out_shape=(
-            jax.ShapeDtypeStruct((GR, TILES * CAP), F32),
-            jax.ShapeDtypeStruct((3, LD, COLS), F32),
-        ),
+        out_shape=(pltpu.VMEM(gate_shape, F32), pltpu.VMEM(incr_shape, F32)),
         in_specs=[pl.BlockSpec(memory_space=pl.ANY)] * 5,
-        out_specs=[pl.BlockSpec(memory_space=pl.ANY)] * 2,
+        out_specs=[pl.BlockSpec(memory_space=pltpu.VMEM)] * 2,
         scratch_shapes=[
             pltpu.VMEM((3, LD, COLS), F32),
             pltpu.VMEM((LD, COLS), F32),
             pltpu.VMEM((1, COLS), jnp.int32),
-            pltpu.VMEM((GR * LEVS, LEV), F32),
+            pltpu.VMEM((LEV, GR * LEVS), F32),
             pltpu.VMEM((GR, TILES * CAP), F32),
-            pltpu.VMEM((GR, TILES * CAP), F32),
-            pltpu.VMEM((3, LD, COLS), F32),
+            pltpu.VMEM((LD, COLS), BF16),
             pltpu.VMEM((3, LD, COLS), F32),
             pltpu.VMEM((2, LD, COLS), BF16),
             pltpu.VMEM((TILES * COLS // CAP, CAP), BF16),
             pltpu.VMEM((TILES * COLS // CAP, 2 * CAP), F32),
-            pltpu.VMEM((CAP, COLS), BF16),
-            pltpu.VMEM((PC * NC * LD, 2 * COLS), BF16),
+            pltpu.VMEM((NC * CAP, COLS), BF16),
+            pltpu.VMEM((2 * PC * LD, COLS), BF16),
             pltpu.VMEM((TILES, *block), F32),
             pltpu.VMEM((LEVS, TILES, *block), F32),
             pltpu.VMEM((2, CHUNKS, HALF * NC, *block), F32),
@@ -392,14 +401,24 @@
             pltpu.VMEM((TILES, *block), F32),
             pltpu.VMEM((LEVS, TILES, *block), F32),
             pltpu.VMEM((LD, COLS), F32),
-            dma((5,)), dma((2,)), dma, dma((CHUNKS,)), dma, dma((CHUNKS,)),
+            pltpu.VMEM((2 * PC * LD, NC * CAP), BF16),
+            dma((5,)), dma, dma((CHUNKS,)), dma, dma((CHUNKS,)),
             dma(per_way), dma(per_way), dma(per_way), dma(per_way),
             dma(per_way), dma(per_way), dma(per_way), dma(per_way),
         ],
         compiler_params=pltpu.CompilerParams(
             collective_id=0, has_side_effects=True, vmem_limit_bytes=48 * 1024 * 1024
         ),
-    )(mixing, density, routes.reshape(1, COLS), beam_weight, gate_adjoint)
+    )(*[pltpu.with_memory_space_constraint(x, pltpu.HBM) for x in operands])
+    return pl.pallas_call(
+        store,
+        out_shape=(
+            jax.ShapeDtypeStruct(gate_shape, F32), jax.ShapeDtypeStruct(incr_shape, F32)
+        ),
+        in_specs=[pl.BlockSpec(memory_space=pl.ANY)] * 2,
+        out_specs=[pl.BlockSpec(memory_space=pl.ANY)] * 2,
+        scratch_shapes=[dma((2,))],
+    )(*[pltpu.with_memory_space_constraint(x, pltpu.VMEM) for x in (gate, incr)])
 
 
 def solution(mesh):

time: 68.9 us -> 53.3 us (0.77)
  Pallas kernels: 60.8 us -> 52.5 us
  local copies, waits for them, and re-layouts: 7.16 us -> 0 us
    pallas_call x1 -> x2, Pallas kernels: 60.8 us -> 52.5 us  [the longest x1 51.1 us: per_device(): pl.pallas_call(kernel, out_shape=(pltpu.VMEM(gate_shape, F32), pltpu.VMEM...]
    unnamed x11 -> x0, local copies, waits for them, and re-layouts: 7.16 us -> none
where the time goes in v2:
time: 53.3 us; the launch traced here: 53.2 us
  Pallas kernels  52.5 us (98%)
  between operations  0.64 us (1%)
    pallas_call x1, Pallas kernels, per_device(): pl.pallas_call(kernel, out_shape=(pltpu.VMEM(gate_shape, F32), pltpu.VMEM...  51.1 us
    pallas_call x1, Pallas kernels, per_device(): pl.pallas_call(store, out_shape=(jax.ShapeDtypeStruct(gate_shape, F32), j...  1.42 us

profile of v2, /device:TPU:1, one launch (start us, length us, event | category | flops | bytes accessed | tf_op | source)
XLA Modules:
  0.0 53.2 jit_solution(2467973058410519166)
XLA Ops:
  0.6 51.1 %shard_map.68 = (f32[42,8192]{1,0:T(8,128)S(1)}, f32[3,16,4096]{2,1,0:T(8,128)S(1)}) custom-call(f32[3,16,4096]{2,1,0:T(8,128)} %mixing_hbm.1, f32[16,4096]{1,0:T(8,128)} %density_hbm.1, s32[1,4096]{1,0:T(1,128)} %bitcast.3, f32[1,64,168]{2,1,0:T(8,128)} %bitcast.2, f32[42,8192]{1,0:T(8,128)} %adjoint_hbm.1), custom_call_target="tpu_custom_call" | custom-call | tf_op jit(solution)/shard_map/pallas_call | solution.py:378
  51.8 1.4 %shard_map.69 = (f32[42,8192]{1,0:T(8,128)}, f32[3,16,4096]{2,1,0:T(8,128)}) custom-call(f32[42,8192]{1,0:T(8,128)S(1)} %get-tuple-element.4.gate, f32[3,16,4096]{2,1,0:T(8,128)S(1)} %get-tuple-element.5.incr), custom_call_target="tpu_custom_call" | custom-call | tf_op jit(solution)/shard_map/pallas_call | solution.py:413

commit v3 on v2

v3 whole, which is shorter than its diff:
```python
import jax
import jax.numpy as jnp
from jax import lax
from jax.experimental import pallas as pl
from jax.experimental.pallas import tpu as pltpu
from jax.sharding import PartitionSpec as P

coefficients = (3.63, 0.96, 1.98)
exponents = (1.75, 1.66, 1.75)

MESH = pl.DeviceIdType.MESH
F32 = jnp.float32
BF16 = jnp.bfloat16

NX, NZ, NC = 4, 8, 2
LEVS = 4
TILES = NX * NZ * NC
PAIRS = NX * NZ
SC = 8
RC = 4
AC = 4
COLS = 4096
LD = 16
LEV = 64
CAP = 128
GR = 42


def split2(value):
    hi = value.astype(BF16)
    lo = (value - hi.astype(F32)).astype(BF16)
    return hi, lo


def dot(a, b, dims=((1,), (0,))):
    return lax.dot_general(a, b, (dims, ((), ())), preferred_element_type=F32)


def shift_of(kp):
    dzi = kp // NX
    dx = kp % NX
    dz = ((dzi + 1) // 2) * (2 * (dzi % 2) - 1)
    return dx, dz


def kernel(
    mixing_hbm, density_hbm, routes_hbm, weight_hbm, adjoint_hbm,
    gate, incr,
    mixing, density, target, weight, adjoint, pair_of,
    slopes, parts, onehot, prefix, ranks1h, lhs, out_blocks,
    partial, rs1, rs2, final, back, cols, restored, got, rows3,
    in_sem, adj_sem, a2a_send, a2a_recv, bk_send, bk_recv,
    rs1_send, rs1_recv, rs2_send, rs2_recv, ag1_send, ag1_recv, ag2_send, ag2_recv, met,
):
    tile = lax.axis_index("tile")
    lev = lax.axis_index("lev")
    core = tile % NC
    zz = (tile // NC) % NZ
    xx = tile // (NC * NZ)
    right = (lev + 1) % LEVS
    left = (lev + 3) % LEVS
    across = (lev + 2) % LEVS

    def pair_plus(kp):
        dx, dz = shift_of(kp)
        return ((xx + dx) % NX) * NZ + (zz + dz + NZ) % NZ

    def pair_minus(kp):
        dx, dz = shift_of(kp)
        return ((xx - dx + NX) % NX) * NZ + (zz - dz + NZ) % NZ

    loads = [
        pltpu.make_async_copy(weight_hbm.at[0], weight, in_sem.at[0]),
        pltpu.make_async_copy(routes_hbm, target, in_sem.at[1]),
        pltpu.make_async_copy(density_hbm, density, in_sem.at[2]),
        pltpu.make_async_copy(mixing_hbm, mixing, in_sem.at[3]),
    ]
    loads[0].start()

    def adjoint_load(c):
        for kp in range(c * SC, (c + 1) * SC):
            at = pl.ds(pl.multiple_of(pair_plus(kp) * NC * CAP, NC * CAP), NC * CAP)
            pltpu.make_async_copy(
                adjoint_hbm.at[:, at], adjoint.at[:, at], adj_sem.at[c]
            ).start()

    adjoint_load(0)

    def adjoint_wait(c):
        some = pl.ds(0, SC * NC * CAP)
        pltpu.make_async_copy(
            adjoint_hbm.at[:, some], adjoint.at[:, some], adj_sem.at[c]
        ).wait()

    def named(dx, dz, dc):
        x, z = (xx + dx + NX) % NX, (zz + dz + NZ) % NZ
        return {"tile": (x * NZ + z) * NC + (core + dc) % NC}

    near_z = [named(0, 1, 0), named(0, -1, 0)]
    near_x = [named(1, 0, 0), named(-1, 0, 0)]
    far_z = [named(0, 2, 0), named(0, -2, 0)]
    far_x = [named(2, 0, 0)]
    twin = [named(0, 0, 1)]

    def tell(sem, peers):
        for peer in peers:
            pl.semaphore_signal(sem, inc=1, device_id=peer, device_id_type=MESH)

    barrier = pltpu.get_barrier_semaphore()
    tell(barrier, [{"lev": left}, {"lev": right}] + near_z + near_x + twin)
    stages = [
        (met.at[0], near_z + near_x),
        (met.at[1], far_z),
        (met.at[2], near_x + far_x),
        (met.at[3], twin),
    ]

    def pass_on(stage):
        if stage > 0:
            sem, peers = stages[stage - 1]
            pl.semaphore_wait(sem, len(peers))
        if stage < len(stages):
            tell(*stages[stage])

    loads[0].wait()
    for c in range(1, PAIRS // SC):
        adjoint_load(c)
    for load in loads[1:]:
        load.start()
    mine = weight[:, :GR]
    for k in range(1, LEVS):
        mine = jnp.where(lev == k, weight[:, GR * k : GR * (k + 1)], mine)
    mine_hi, mine_lo = split2(mine)
    def adjoint_pair(kp):
        at = pl.multiple_of(pair_plus(kp) * 2 * CAP, 2 * CAP)
        g_hi, g_lo = split2(adjoint[:, pl.ds(at, 2 * CAP)])
        part = dot(mine_hi, g_hi) + dot(mine_hi, g_lo) + dot(mine_lo, g_hi)
        for k in range(LEVS):
            for c in range(NC):
                partial[k, kp * NC + c] = part[LD * k : LD * (k + 1), CAP * c : CAP * (c + 1)]

    def lev_copy(src, dst, send, recv, peer):
        return pltpu.make_async_remote_copy(
            src_ref=src, dst_ref=dst, send_sem=send, recv_sem=recv,
            device_id={"lev": peer}, device_id_type=MESH,
        )

    def blocks(buf, count, send, recv):
        some = buf.at[pl.ds(0, count)]
        return pltpu.make_async_remote_copy(
            src_ref=some, dst_ref=some, send_sem=send, recv_sem=recv,
            device_id={"lev": right}, device_id_type=MESH,
        )

    def rs1_copy(c, way):
        at = (c * RC + way * (RC // 2)) * NC
        return lev_copy(
            partial.at[across, pl.ds(at, RC // 2 * NC)], rs1.at[way, c],
            rs1_send, rs1_recv.at[c], (right, left)[way],
        )

    def rs2_copy(c, way):
        peer = (right, left)[way]
        return lev_copy(
            partial.at[peer, pl.ds(c * RC * NC, RC * NC)], rs2.at[way, c],
            rs2_send, rs2_recv.at[c], peer,
        )

    def ag1_copy(c, way):
        here = cols.at[lev, pl.ds(c * AC * NC, AC * NC)]
        return lev_copy(
            here, here, ag1_send, ag1_recv.at[c], (right, left)[way]
        )

    def ag2_copy(c, way):
        at = (c * AC + way * (AC // 2)) * NC
        here = cols.at[(left, right)[way], pl.ds(at, AC // 2 * NC)]
        return lev_copy(
            here, here, ag2_send, ag2_recv.at[c], (right, left)[way]
        )

    def adjoint_sums(c):
        for kp in range(c * RC, (c + 1) * RC):
            adjoint_pair(kp)

    def rs_first(c):
        for way in range(2):
            rs1_copy(c, way).start()

    def rs_second(c):
        blocks(final, RC * NC, rs1_send, rs1_recv.at[c]).wait_recv()
        for way in range(2):
            peer = (right, left)[way]
            at = pl.ds((c * RC + way * (RC // 2)) * NC, RC // 2 * NC)
            partial[peer, at] = partial[peer, at] + rs1[way, c]
        for way in range(2):
            rs2_copy(c, way).start()

    def back_copy(kp, cs):
        return pltpu.make_async_remote_copy(
            src_ref=final.at[kp * NC + cs], dst_ref=back.at[kp * NC + core],
            send_sem=bk_send, recv_sem=bk_recv.at[kp // SC],
            device_id={"tile": pair_plus(kp) * NC + cs}, device_id_type=MESH,
        )

    def out_copy(kp, cd):
        return pltpu.make_async_remote_copy(
            src_ref=out_blocks.at[kp * NC + cd], dst_ref=cols.at[lev, kp * NC + core],
            send_sem=a2a_send, recv_sem=a2a_recv.at[kp // AC],
            device_id={"tile": pair_minus(kp) * NC + cd}, device_id_type=MESH,
        )

    def exchange(copy_of, first, count):
        if first == 0:
            copy_of(0, 1 - core).start()

        @pl.loop(max(first, 1), first + count, unroll=4)
        def _(kp):
            for other in range(NC):
                copy_of(kp, other).start()

    def in_chunk(pairs, c):
        return pairs * NC - (1 if c == 0 else 0)

    def rs_final(c):
        blocks(final, 2 * RC * NC, rs2_send, rs2_recv.at[c]).wait_recv()
        at = pl.ds(c * RC * NC, RC * NC)
        final[at] = partial[lev, at] + rs2[0, c] + rs2[1, c]

    adjoint_wait(0)
    adjoint_sums(0)
    pl.semaphore_wait(barrier, 7)
    pass_on(0)
    rs_first(0)
    for c in range(1, PAIRS // RC):
        if c * RC % SC == 0:
            adjoint_wait(c * RC // SC)
        adjoint_sums(c)
        rs_first(c)
        if c == 4:
            pass_on(1)

    loads[1].wait()
    for j in range(COLS // CAP):
        names = lax.broadcasted_iota(jnp.int32, (TILES, CAP), 0)
        onehot[TILES * j : TILES * (j + 1), :] = jnp.where(
            target[:, CAP * j : CAP * (j + 1)] == names, 1.0, 0.0
        ).astype(BF16)
    upto = jnp.where(
        lax.broadcasted_iota(jnp.int32, (CAP, 2 * CAP), 0)
        < lax.broadcasted_iota(jnp.int32, (CAP, 2 * CAP), 1),
        1.0, 0.0,
    ).astype(BF16)
    prefix[...] = dot(onehot[...], upto)
    carry = jnp.zeros((TILES, CAP), F32)
    slot = lax.broadcasted_iota(jnp.int32, (NC * CAP, CAP), 0).astype(F32)
    for j in range(COLS // CAP):
        at = slice(TILES * j, TILES * (j + 1))
        before = onehot[at, :].astype(F32) * (prefix[at, :CAP] + carry)
        odd = (target[:, CAP * j : CAP * (j + 1)] % NC).astype(F32)
        rank = jnp.sum(before, axis=0, keepdims=True) + CAP * odd
        ranks1h[:, CAP * j : CAP * (j + 1)] = jnp.where(rank == slot, 1.0, 0.0).astype(BF16)
        carry = carry + prefix[at, CAP:]

    pair_of[...] = jnp.broadcast_to((target[...] // NC).astype(F32), (LD, COLS)).astype(BF16)

    pass_on(2)

    loads[2].wait()
    loads[3].wait()
    wide = 512

    @pl.loop(0, COLS // wide, unroll=2)
    def _(j):
        at = pl.ds(pl.multiple_of(j * wide, wide), wide)
        dens = density[:, at]
        summed = jnp.zeros((LD, wide), F32)
        for species in range(3):
            mix = mixing[species, :, at]
            powered = coefficients[species] * jnp.exp(exponents[species] * jnp.log(dens * mix))
            summed = summed + powered
            slopes[species, :, at] = exponents[species] * powered / mix
        hi, lo = split2(summed)
        parts[0, :, at] = hi
        parts[1, :, at] = lo


    rows_hi, rows_lo = split2(mine.T)
    rows3[...] = jnp.concatenate([rows_hi, rows_hi, rows_lo], axis=1)

    def build(c):
        zero = jnp.zeros((), BF16)
        for i in range(SC):
            pair = pair_minus(c * SC + i)
            same = pair_of[...] == pair.astype(F32).astype(BF16)
            for p in range(2):
                at = (p * SC + i) * LD
                lhs[at : at + LD, :] = jnp.where(same, parts[p], zero)

    def place(c):
        both = dot(lhs[...], ranks1h[...], ((1,), (1,)))
        placed = both[: SC * LD] + both[SC * LD :]
        for i in range(SC):
            for cd in range(NC):
                out_blocks[(c * SC + i) * NC + cd] = placed[
                    i * LD : (i + 1) * LD, cd * CAP : (cd + 1) * CAP
                ]
        if c == 0:
            cols[lev, core] = out_blocks[core]

    def ag_first(c):
        blocks(out_blocks, in_chunk(AC, c), a2a_send, a2a_recv.at[c]).wait_recv()
        for way in range(2):
            ag1_copy(c, way).start()

    def ag_second(c):
        blocks(final, 2 * AC * NC, ag1_send, ag1_recv.at[c]).wait_recv()
        for way in range(2):
            ag2_copy(c, way).start()

    def gates(c):
        blocks(final, AC * NC, ag2_send, ag2_recv.at[c]).wait_recv()

        @pl.loop(c * AC, (c + 1) * AC, unroll=AC)
        def _(kp):
            both = [cols[:, kp * NC + cs].reshape(LEV, CAP) for cs in range(NC)]
            x_hi, x_lo = split2(jnp.concatenate(both, axis=1))
            at = pl.multiple_of(pair_plus(kp) * 2 * CAP, 2 * CAP)
            gate[:, pl.ds(at, 2 * CAP)] = dot(
                rows3[...], jnp.concatenate([x_hi, x_lo, x_hi], axis=0)
            )

    def gather(c):
        blocks(final, in_chunk(SC, c), bk_send, bk_recv.at[c]).wait_recv()
        if c == 0:
            back[core] = final[core]
        span = SC * LD
        for i in range(SC):
            two = [back[(c * SC + i) * NC + cd] for cd in range(NC)]
            b_hi, b_lo = split2(jnp.concatenate(two, axis=1))
            got[i * LD : (i + 1) * LD, :] = b_hi
            got[span + i * LD : span + (i + 1) * LD, :] = b_lo

        @pl.loop(0, COLS // wide, unroll=2)
        def _(j):
            at = pl.ds(pl.multiple_of(j * wide, wide), wide)
            twice = dot(got[...], ranks1h[:, at])
            spread = twice[:span] + twice[span:]
            names = jnp.broadcast_to(target[:, at] // NC, (LD, wide))
            if c == 0:
                total = jnp.zeros((LD, wide), F32)
            else:
                total = restored[:, at]
            for i in range(SC):
                mine = spread[i * LD : (i + 1) * LD]
                total = jnp.where(names == pair_minus(c * SC + i), mine, total)
            if c < PAIRS // SC - 1:
                restored[:, at] = total
            else:
                for species in range(3):
                    incr[species, :, at] = slopes[species, :, at] * total

    def rs_return(c):
        rs_final(c)
        exchange(back_copy, c * RC, RC)

    rs_second(0)
    pass_on(3)
    build(0)
    rs_second(1)
    place(0)
    rs_second(2)
    pass_on(4)
    exchange(out_copy, 0, SC)
    rs_second(3)
    build(1)
    rs_second(4)
    place(1)
    exchange(out_copy, SC, SC)
    rs_second(5)
    build(2)
    rs_second(6)
    place(2)
    exchange(out_copy, 2 * SC, SC)
    rs_second(7)
    build(3)
    place(3)
    exchange(out_copy, 3 * SC, SC)
    for c in range(5):
        rs_return(c)
    ag_first(0)
    rs_return(5)
    ag_first(1)
    rs_return(6)
    ag_first(2)
    ag_first(3)
    rs_return(7)
    ag_first(4)
    ag_second(0)
    ag_first(5)
    ag_second(1)
    ag_first(6)
    ag_first(7)
    ag_second(2)
    gather(0)
    ag_second(3)
    gates(0)
    ag_second(4)
    gather(1)
    ag_second(5)
    gates(1)
    ag_second(6)
    ag_second(7)
    gather(2)
    gates(2)
    gates(3)
    gates(4)
    gather(3)
    gates(5)
    gates(6)
    gates(7)

    def finish():
        blocks(final, TILES, rs1_send, rs1_recv.at[0]).wait_send()
        blocks(final, TILES, ag2_send, ag2_recv.at[0]).wait_send()
        for sem in (rs2_send, ag1_send):
            both = cols.at[pl.ds(0, 2)]
            lev_copy(both, both, sem, ag1_recv.at[0], right).wait_send()
        blocks(out_blocks, TILES - 1, a2a_send, a2a_recv.at[0]).wait_send()
        blocks(final, TILES - 1, bk_send, bk_recv.at[0]).wait_send()

    finish()


def store(gate, incr, gate_hbm, incr_hbm, sem):
    pieces, wide = 4, TILES * CAP // 4
    copies = []
    for i in range(pieces):
        at = pl.ds(i * wide, wide)
        copies.append(pltpu.make_async_copy(gate.at[:, at], gate_hbm.at[:, at], sem.at[i]))
    for i in range(3):
        copies.append(pltpu.make_async_copy(incr.at[i], incr_hbm.at[i], sem.at[pieces + i]))
    for copy in copies:
        copy.start()
    for copy in copies:
        copy.wait()


def per_device(mixing, density, routes, beam_weight, gate_adjoint):
    dma = pltpu.SemaphoreType.DMA
    block = (LD, CAP)
    rs_way = (2, PAIRS // RC)
    gate_shape, incr_shape = (GR, TILES * CAP), (3, LD, COLS)
    operands = (
        mixing, density, routes.reshape(1, COLS),
        jnp.swapaxes(beam_weight, 1, 2), gate_adjoint,
    )
    gate, incr = pl.pallas_call(
        kernel,
        out_shape=(pltpu.VMEM(gate_shape, F32), pltpu.VMEM(incr_shape, F32)),
        in_specs=[pl.BlockSpec(memory_space=pl.ANY)] * 5,
        out_specs=[pl.BlockSpec(memory_space=pltpu.VMEM)] * 2,
        scratch_shapes=[
            pltpu.VMEM((3, LD, COLS), F32),
            pltpu.VMEM((LD, COLS), F32),
            pltpu.VMEM((1, COLS), jnp.int32),
            pltpu.VMEM((LEV, GR * LEVS), F32),
            pltpu.VMEM((GR, TILES * CAP), F32),
            pltpu.VMEM((LD, COLS), BF16),
            pltpu.VMEM((3, LD, COLS), F32),
            pltpu.VMEM((2, LD, COLS), BF16),
            pltpu.VMEM((TILES * COLS // CAP, CAP), BF16),
            pltpu.VMEM((TILES * COLS // CAP, 2 * CAP), F32),
            pltpu.VMEM((NC * CAP, COLS), BF16),
            pltpu.VMEM((2 * SC * LD, COLS), BF16),
            pltpu.VMEM((TILES, *block), F32),
            pltpu.VMEM((LEVS, TILES, *block), F32),
            pltpu.VMEM((*rs_way, RC // 2 * NC, *block), F32),
            pltpu.VMEM((*rs_way, RC * NC, *block), F32),
            pltpu.VMEM((TILES, *block), F32),
            pltpu.VMEM((TILES, *block), F32),
            pltpu.VMEM((LEVS, TILES, *block), F32),
            pltpu.VMEM((LD, COLS), F32),
            pltpu.VMEM((2 * SC * LD, NC * CAP), BF16),
            pltpu.VMEM((GR, 3 * LEV), BF16),
            dma((4,)), dma((PAIRS // SC,)), dma, dma((PAIRS // AC,)), dma, dma((PAIRS // SC,)),
            dma, dma((PAIRS // RC,)), dma, dma((PAIRS // RC,)),
            dma, dma((PAIRS // AC,)), dma, dma((PAIRS // AC,)),
            pltpu.SemaphoreType.REGULAR((4,)),
        ],
        compiler_params=pltpu.CompilerParams(
            collective_id=0, has_side_effects=True, vmem_limit_bytes=48 * 1024 * 1024
        ),
    )(*[pltpu.with_memory_space_constraint(x, pltpu.HBM) for x in operands])
    return pl.pallas_call(
        store,
        out_shape=(
            jax.ShapeDtypeStruct(gate_shape, F32), jax.ShapeDtypeStruct(incr_shape, F32)
        ),
        in_specs=[pl.BlockSpec(memory_space=pl.ANY)] * 2,
        out_specs=[pl.BlockSpec(memory_space=pl.ANY)] * 2,
        scratch_shapes=[dma((7,))],
    )(*[pltpu.with_memory_space_constraint(x, pltpu.VMEM) for x in (gate, incr)])


def solution(mesh):
    return jax.shard_map(
        per_device,
        mesh=mesh,
        in_specs=(
            P(None, "lev", "tile"),
            P("lev", "tile"),
            P("tile", None),
            P("tile", None, None),
            P("lev", "tile"),
        ),
        out_specs=(P("lev", "tile"), P(None, "lev", "tile")),
        check_vma=False,
    )
```

time: 53.3 us -> 48.9 us (0.917)
  Pallas kernels: 52.5 us -> 48.1 us
    pallas_call x1, Pallas kernels: 51.1 us -> 46.6 us  [per_device(): pl.pallas_call(kernel, out_shape=(pltpu.VMEM(gate_shape, F32), pltpu.VMEM...]
where the time goes in v3:
time: 48.9 us; the launch traced here: 48.7 us
  Pallas kernels  48.1 us (98%)
  between operations  0.64 us (1%)
    pallas_call x1, Pallas kernels, per_device(): pl.pallas_call(kernel, out_shape=(pltpu.VMEM(gate_shape, F32), pltpu.VMEM...  46.6 us
    pallas_call x1, Pallas kernels, per_device(): pl.pallas_call(store, out_shape=(jax.ShapeDtypeStruct(gate_shape, F32), j...  1.46 us

profile of v3, /device:TPU:1, one launch (start us, length us, event | category | flops | bytes accessed | tf_op | source)
XLA Modules:
  0.0 48.7 jit_solution(12871449244191259698)
XLA Ops:
  0.6 46.6 %shard_map.68 = (f32[42,8192]{1,0:T(8,128)S(1)}, f32[3,16,4096]{2,1,0:T(8,128)S(1)}) custom-call(f32[3,16,4096]{2,1,0:T(8,128)} %mixing_hbm.1, f32[16,4096]{1,0:T(8,128)} %density_hbm.1, s32[1,4096]{1,0:T(1,128)} %bitcast.3, f32[1,64,168]{2,1,0:T(8,128)} %bitcast.2, f32[42,8192]{1,0:T(8,128)} %adjoint_hbm.1), custom_call_target="tpu_custom_call" | custom-call | tf_op jit(solution)/shard_map/pallas_call | solution.py:458
  47.3 1.5 %shard_map.69 = (f32[42,8192]{1,0:T(8,128)}, f32[3,16,4096]{2,1,0:T(8,128)}) custom-call(f32[42,8192]{1,0:T(8,128)S(1)} %get-tuple-element.4.gate, f32[3,16,4096]{2,1,0:T(8,128)S(1)} %get-tuple-element.5.incr), custom_call_target="tpu_custom_call" | custom-call | tf_op jit(solution)/shard_map/pallas_call | solution.py:495

commit v4 on v3

--- a/solution.py
+++ b/solution.py
@@ -17,8 +17,10 @@
 TILES = NX * NZ * NC
 PAIRS = NX * NZ
 SC = 8
+QC = 8
 RC = 4
 AC = 4
+OWN = NX
 COLS = 4096
 LD = 16
 LEV = 64
@@ -39,7 +41,7 @@
 def shift_of(kp):
     dzi = kp // NX
     dx = kp % NX
-    dz = ((dzi + 1) // 2) * (2 * (dzi % 2) - 1)
+    dz = (4 - dzi // 2) * (1 - 2 * (dzi % 2)) + 4 * ((8 - dzi) // 7 - (8 - dzi) // 8)
     return dx, dz
 
 
@@ -96,23 +98,23 @@
         x, z = (xx + dx + NX) % NX, (zz + dz + NZ) % NZ
         return {"tile": (x * NZ + z) * NC + (core + dc) % NC}
 
-    near_z = [named(0, 1, 0), named(0, -1, 0)]
-    near_x = [named(1, 0, 0), named(-1, 0, 0)]
+    near = [named(0, 1, 0), named(0, -1, 0), named(1, 0, 0), named(-1, 0, 0)]
     far_z = [named(0, 2, 0), named(0, -2, 0)]
-    far_x = [named(2, 0, 0)]
+    all_x = [named(1, 0, 0), named(2, 0, 0), named(3, 0, 0)]
+    twin_x = [named(1, 0, 1), named(2, 0, 1), named(3, 0, 1)]
     twin = [named(0, 0, 1)]
+    first = [{"lev": left}, {"lev": right}] + near + twin
 
     def tell(sem, peers):
         for peer in peers:
             pl.semaphore_signal(sem, inc=1, device_id=peer, device_id_type=MESH)
 
     barrier = pltpu.get_barrier_semaphore()
-    tell(barrier, [{"lev": left}, {"lev": right}] + near_z + near_x + twin)
+    tell(barrier, first)
     stages = [
-        (met.at[0], near_z + near_x),
-        (met.at[1], far_z),
-        (met.at[2], near_x + far_x),
-        (met.at[3], twin),
+        (met.at[0], near),
+        (met.at[1], far_z + all_x),
+        (met.at[2], all_x + twin_x + twin),
     ]
 
     def pass_on(stage):
@@ -211,16 +213,22 @@
         )
 
     def exchange(copy_of, first, count):
-        if first == 0:
-            copy_of(0, 1 - core).start()
-
-        @pl.loop(max(first, 1), first + count, unroll=4)
-        def _(kp):
-            for other in range(NC):
-                copy_of(kp, other).start()
+        def pairs(at, number):
+            @pl.loop(at, at + number, unroll=min(4, number))
+            def _(kp):
+                for other in range(NC):
+                    copy_of(kp, other).start()
+
+        if first <= OWN < first + count:
+            if first < OWN:
+                pairs(first, OWN - first)
+            copy_of(OWN, 1 - core).start()
+            pairs(OWN + 1, first + count - OWN - 1)
+        else:
+            pairs(first, count)
 
     def in_chunk(pairs, c):
-        return pairs * NC - (1 if c == 0 else 0)
+        return pairs * NC - (1 if c == OWN // pairs else 0)
 
     def rs_final(c):
         blocks(final, 2 * RC * NC, rs2_send, rs2_recv.at[c]).wait_recv()
@@ -229,7 +237,7 @@
 
     adjoint_wait(0)
     adjoint_sums(0)
-    pl.semaphore_wait(barrier, 7)
+    pl.semaphore_wait(barrier, len(first))
     pass_on(0)
     rs_first(0)
     for c in range(1, PAIRS // RC):
@@ -237,8 +245,7 @@
             adjoint_wait(c * RC // SC)
         adjoint_sums(c)
         rs_first(c)
-        if c == 4:
-            pass_on(1)
+    pass_on(1)
 
     loads[1].wait()
     for j in range(COLS // CAP):
@@ -253,18 +260,20 @@
     ).astype(BF16)
     prefix[...] = dot(onehot[...], upto)
     carry = jnp.zeros((TILES, CAP), F32)
-    slot = lax.broadcasted_iota(jnp.int32, (NC * CAP, CAP), 0).astype(F32)
+    slot = lax.broadcasted_iota(jnp.int32, (NC * CAP, CAP), 0).astype(F32).astype(BF16)
+    one, zero = jnp.ones((), BF16), jnp.zeros((), BF16)
     for j in range(COLS // CAP):
         at = slice(TILES * j, TILES * (j + 1))
         before = onehot[at, :].astype(F32) * (prefix[at, :CAP] + carry)
         odd = (target[:, CAP * j : CAP * (j + 1)] % NC).astype(F32)
         rank = jnp.sum(before, axis=0, keepdims=True) + CAP * odd
-        ranks1h[:, CAP * j : CAP * (j + 1)] = jnp.where(rank == slot, 1.0, 0.0).astype(BF16)
+        ranks1h[:, CAP * j : CAP * (j + 1)] = jnp.where(
+            jnp.broadcast_to(rank.astype(BF16), slot.shape) == slot, one, zero
+        )
         carry = carry + prefix[at, CAP:]
 
     pair_of[...] = jnp.broadcast_to((target[...] // NC).astype(F32), (LD, COLS)).astype(BF16)
 
-    pass_on(2)
 
     loads[2].wait()
     loads[3].wait()
@@ -289,24 +298,25 @@
     rows3[...] = jnp.concatenate([rows_hi, rows_hi, rows_lo], axis=1)
 
     def build(c):
-        zero = jnp.zeros((), BF16)
         for i in range(SC):
             pair = pair_minus(c * SC + i)
             same = pair_of[...] == pair.astype(F32).astype(BF16)
             for p in range(2):
-                at = (p * SC + i) * LD
+                at = (i // QC * 2 * QC + p * QC + i % QC) * LD
                 lhs[at : at + LD, :] = jnp.where(same, parts[p], zero)
 
     def place(c):
-        both = dot(lhs[...], ranks1h[...], ((1,), (1,)))
-        placed = both[: SC * LD] + both[SC * LD :]
-        for i in range(SC):
-            for cd in range(NC):
-                out_blocks[(c * SC + i) * NC + cd] = placed[
-                    i * LD : (i + 1) * LD, cd * CAP : (cd + 1) * CAP
-                ]
-        if c == 0:
-            cols[lev, core] = out_blocks[core]
+        for q in range(SC // QC):
+            rows = 2 * QC * LD
+            both = dot(lhs[q * rows : (q + 1) * rows], ranks1h[...], ((1,), (1,)))
+            placed = both[: QC * LD] + both[QC * LD :]
+            for i in range(QC):
+                for cd in range(NC):
+                    out_blocks[(c * SC + q * QC + i) * NC + cd] = placed[
+                        i * LD : (i + 1) * LD, cd * CAP : (cd + 1) * CAP
+                    ]
+        if c == OWN // SC:
+            cols[lev, OWN * NC + core] = out_blocks[OWN * NC + core]
 
     def ag_first(c):
         blocks(out_blocks, in_chunk(AC, c), a2a_send, a2a_recv.at[c]).wait_recv()
@@ -332,8 +342,8 @@
 
     def gather(c):
         blocks(final, in_chunk(SC, c), bk_send, bk_recv.at[c]).wait_recv()
-        if c == 0:
-            back[core] = final[core]
+        if c == OWN // SC:
+            back[OWN * NC + core] = final[OWN * NC + core]
         span = SC * LD
         for i in range(SC):
             two = [back[(c * SC + i) * NC + cd] for cd in range(NC)]
@@ -341,7 +351,7 @@
             got[i * LD : (i + 1) * LD, :] = b_hi
             got[span + i * LD : span + (i + 1) * LD, :] = b_lo
 
-        @pl.loop(0, COLS // wide, unroll=2)
+        @pl.loop(0, COLS // wide, unroll=4)
         def _(j):
             at = pl.ds(pl.multiple_of(j * wide, wide), wide)
             twice = dot(got[...], ranks1h[:, at])
@@ -364,13 +374,13 @@
         rs_final(c)
         exchange(back_copy, c * RC, RC)
 
+    pass_on(2)
     rs_second(0)
-    pass_on(3)
     build(0)
     rs_second(1)
     place(0)
     rs_second(2)
-    pass_on(4)
+    pass_on(3)
     exchange(out_copy, 0, SC)
     rs_second(3)
     build(1)
@@ -402,20 +412,20 @@
     ag_first(6)
     ag_first(7)
     ag_second(2)
+    ag_second(3)
+    ag_second(4)
     gather(0)
-    ag_second(3)
+    ag_second(5)
     gates(0)
-    ag_second(4)
+    ag_second(6)
     gather(1)
-    ag_second(5)
+    ag_second(7)
     gates(1)
-    ag_second(6)
-    ag_second(7)
     gather(2)
     gates(2)
     gates(3)
+    gather(3)
     gates(4)
-    gather(3)
     gates(5)
     gates(6)
     gates(7)
@@ -486,7 +496,7 @@
             dma((4,)), dma((PAIRS // SC,)), dma, dma((PAIRS // AC,)), dma, dma((PAIRS // SC,)),
             dma, dma((PAIRS // RC,)), dma, dma((PAIRS // RC,)),
             dma, dma((PAIRS // AC,)), dma, dma((PAIRS // AC,)),
-            pltpu.SemaphoreType.REGULAR((4,)),
+            pltpu.SemaphoreType.REGULAR((3,)),
         ],
         compiler_params=pltpu.CompilerParams(
             collective_id=0, has_side_effects=True, vmem_limit_bytes=48 * 1024 * 1024

time: 48.9 us -> 46.4 us (0.949)
  Pallas kernels: 48.1 us -> 45.6 us
    pallas_call x1, Pallas kernels: 46.6 us -> 44.2 us  [per_device(): pl.pallas_call(kernel, out_shape=(pltpu.VMEM(gate_shape, F32), pltpu.VMEM...]
where the time goes in v4:
time: 46.4 us; the launch traced here: 46.3 us
  Pallas kernels  45.6 us (98%)
  between operations  0.64 us (1%)
    pallas_call x1, Pallas kernels, per_device(): pl.pallas_call(kernel, out_shape=(pltpu.VMEM(gate_shape, F32), pltpu.VMEM...  44.2 us
    pallas_call x1, Pallas kernels, per_device(): pl.pallas_call(store, out_shape=(jax.ShapeDtypeStruct(gate_shape, F32), j...  1.46 us

profile of v4, /device:TPU:1, one launch (start us, length us, event | category | flops | bytes accessed | tf_op | source)
XLA Modules:
  0.0 46.3 jit_solution(11386016551841569136)
XLA Ops:
  0.6 44.2 %shard_map.68 = (f32[42,8192]{1,0:T(8,128)S(1)}, f32[3,16,4096]{2,1,0:T(8,128)S(1)}) custom-call(f32[3,16,4096]{2,1,0:T(8,128)} %mixing_hbm.1, f32[16,4096]{1,0:T(8,128)} %density_hbm.1, s32[1,4096]{1,0:T(1,128)} %bitcast.3, f32[1,64,168]{2,1,0:T(8,128)} %bitcast.2, f32[42,8192]{1,0:T(8,128)} %adjoint_hbm.1), custom_call_target="tpu_custom_call" | custom-call | tf_op jit(solution)/shard_map/pallas_call | solution.py:468
  44.8 1.5 %shard_map.69 = (f32[42,8192]{1,0:T(8,128)}, f32[3,16,4096]{2,1,0:T(8,128)}) custom-call(f32[42,8192]{1,0:T(8,128)S(1)} %get-tuple-element.4.gate, f32[3,16,4096]{2,1,0:T(8,128)S(1)} %get-tuple-element.5.incr), custom_call_target="tpu_custom_call" | custom-call | tf_op jit(solution)/shard_map/pallas_call | solution.py:505

commit v5 on v4

--- a/solution.py
+++ b/solution.py
@@ -213,19 +213,13 @@
         )
 
     def exchange(copy_of, first, count):
-        def pairs(at, number):
-            @pl.loop(at, at + number, unroll=min(4, number))
-            def _(kp):
+        for i in range(count):
+            kp = first + i % 2 * (count // 2) + i // 2
+            if kp == OWN:
+                copy_of(kp, 1 - core).start()
+            else:
                 for other in range(NC):
                     copy_of(kp, other).start()
-
-        if first <= OWN < first + count:
-            if first < OWN:
-                pairs(first, OWN - first)
-            copy_of(OWN, 1 - core).start()
-            pairs(OWN + 1, first + count - OWN - 1)
-        else:
-            pairs(first, count)
 
     def in_chunk(pairs, c):
         return pairs * NC - (1 if c == OWN // pairs else 0)
@@ -443,7 +437,7 @@
 
 
 def store(gate, incr, gate_hbm, incr_hbm, sem):
-    pieces, wide = 4, TILES * CAP // 4
+    pieces, wide = 2, TILES * CAP // 2
     copies = []
     for i in range(pieces):
         at = pl.ds(i * wide, wide)
@@ -509,7 +503,7 @@
         ),
         in_specs=[pl.BlockSpec(memory_space=pl.ANY)] * 2,
         out_specs=[pl.BlockSpec(memory_space=pl.ANY)] * 2,
-        scratch_shapes=[dma((7,))],
+        scratch_shapes=[dma((5,))],
     )(*[pltpu.with_memory_space_constraint(x, pltpu.VMEM) for x in (gate, incr)])
 
 

time: 46.4 us -> 46.6 us (level)
  no operation moved by 1% of the time
where the time goes in v5:
time: 46.6 us; the launch traced here: 46.4 us
  Pallas kernels  45.8 us (98%)
  between operations  0.64 us (1%)
    pallas_call x1, Pallas kernels, per_device(): pl.pallas_call(kernel, out_shape=(pltpu.VMEM(gate_shape, F32), pltpu.VMEM...  44.3 us
    pallas_call x1, Pallas kernels, per_device(): pl.pallas_call(store, out_shape=(jax.ShapeDtypeStruct(gate_shape, F32), j...  1.44 us

profile of v5, /device:TPU:1, one launch (start us, length us, event | category | flops | bytes accessed | tf_op | source)
XLA Modules:
  0.0 46.4 jit_solution(3914369921940064502)
XLA Ops:
  0.6 44.3 %shard_map.68 = (f32[42,8192]{1,0:T(8,128)S(1)}, f32[3,16,4096]{2,1,0:T(8,128)S(1)}) custom-call(f32[3,16,4096]{2,1,0:T(8,128)} %mixing_hbm.1, f32[16,4096]{1,0:T(8,128)} %density_hbm.1, s32[1,4096]{1,0:T(1,128)} %bitcast.3, f32[1,64,168]{2,1,0:T(8,128)} %bitcast.2, f32[42,8192]{1,0:T(8,128)} %adjoint_hbm.1), custom_call_target="tpu_custom_call" | custom-call | tf_op jit(solution)/shard_map/pallas_call | solution.py:462
  45.0 1.4 %shard_map.69 = (f32[42,8192]{1,0:T(8,128)}, f32[3,16,4096]{2,1,0:T(8,128)}) custom-call(f32[42,8192]{1,0:T(8,128)S(1)} %get-tuple-element.4.gate, f32[3,16,4096]{2,1,0:T(8,128)S(1)} %get-tuple-element.5.incr), custom_call_target="tpu_custom_call" | custom-call | tf_op jit(solution)/shard_map/pallas_call | solution.py:499
